TPU v7x, 32 devices: a whole 2x2x4 slice. The times are simulated.
32 devices in a mesh: seq: 4 (over x, core), mp: 8 (over z, y).
Axes of the slice: x: 2, y: 2, z: 4, core: 2. Of those that a mesh axis runs over, the one named last changes fastest.
Arguments:
- byte_states: bfloat16 [4, 4096, 1024], P('seq', 'mp'), may hold values from -312 to 312
- patch_latents: bfloat16 [4, 1024, 4096], P(None, 'seq', 'mp'), may hold values from -6 to 6
- patch_lengths: int32 [4, 1024], P('seq'), may hold values from 1 to 12, 4096 in all within a row
- w_down: bfloat16 [4096, 1024], replicated, may hold values from -0.09375 to 0.09375
- kv_gain: bfloat16 [1024], replicated, may hold values from 0.25 to 1.75
- w_query: bfloat16 [1024, 1024], replicated, may hold values from -0.375 to 0.375
- w_key: bfloat16 [1024, 1024], replicated, may hold values from -0.1875 to 0.1875
- w_value: bfloat16 [1024, 1024], replicated, may hold values from -0.1875 to 0.1875
- w_out: bfloat16 [1024, 1024], replicated, may hold values from -0.375 to 0.375
- out_gain: bfloat16 [1024], replicated, may hold values from 0.25 to 1.75
Outputs:
- decoded: bfloat16 [4, 4096, 1024], P('seq', 'mp')
Inputs may be any that keep to these rules, and one draw needn't show every extreme that they name: patch_lengths[s] lists the lengths of the 1024 patches of sequence s in order; they sum to 4096 and the longest is exactly 12.
All inputs are finite; a program needn't handle non-finite values.
Results may differ from a plain program's by a relative error of at most 0.0076.
Values may be sent and summed in bfloat16 or wider, within the bound.
A program may use at most 128 MiB of HBM per device.

v0:
```python
import math
import jax
import jax.numpy as jnp
from jax import lax
from jax.sharding import PartitionSpec as P

HEADS = 16
HEAD_DIM = 64
NEG_FLOOR = -1e30


def rms_norm(values, gain_row):
    mean_square = jnp.mean(values * values, axis=-1, keepdims=True)
    return values * lax.rsqrt(mean_square + 1e-05) * gain_row.astype(jnp.float32)


def fold_block(fold_state, query_part, position_part, key_block, value_block, start_block):
    row_max, denominator, accumulated = fold_state
    scale_factor = 1.0 / math.sqrt(HEAD_DIM)
    scores = (
        jnp.einsum("rhd,khd->hrk", query_part, key_block, preferred_element_type=jnp.float32)
        * scale_factor
    )
    allowed = start_block[None, None, :] <= position_part[None, :, None]
    masked = jnp.where(allowed, scores, NEG_FLOOR)
    new_max = jnp.maximum(row_max, jnp.max(masked, axis=-1))
    raised = jnp.where(allowed, jnp.exp(masked - new_max[..., None]), 0.0)
    correction = jnp.exp(row_max - new_max)
    denominator = denominator * correction + jnp.sum(raised, axis=-1)
    accumulated = accumulated * correction[..., None] + jnp.einsum(
        "hrk,khd->hrd", raised.astype(jnp.bfloat16), value_block, preferred_element_type=jnp.float32
    )
    return (new_max, denominator, accumulated)


def make_folder(query_halves, position_halves, starts):

    def folder(running, arrived_piece, piece_start):
        key_piece, value_piece = arrived_piece
        piece_rows = key_piece.shape[0]
        step_rows = math.gcd(piece_rows, 512)

        def one_block(block_index, fold_state):
            offset = block_index * step_rows
            key_block = lax.dynamic_slice_in_dim(key_piece, offset, step_rows, 0).reshape(
                step_rows, HEADS, HEAD_DIM
            )
            value_block = lax.dynamic_slice_in_dim(value_piece, offset, step_rows, 0).reshape(
                step_rows, HEADS, HEAD_DIM
            )
            start_block = lax.dynamic_slice_in_dim(starts, offset, step_rows, 0)
            updated = []
            for part_index in range(2):
                part_state = tuple((member[part_index] for member in fold_state))

                def advance(inner_state, part_index=part_index):
                    return fold_block(
                        inner_state,
                        query_halves[part_index],
                        position_halves[part_index],
                        key_block,
                        value_block,
                        start_block,
                    )

                def remain(inner_state):
                    return inner_state

                needed = start_block[0] <= position_halves[part_index][-1]
                updated.append(lax.cond(needed, advance, remain, part_state))
            return tuple((jnp.stack([updated[0][slot], updated[1][slot]]) for slot in range(3)))

        return lax.fori_loop(0, piece_rows // step_rows, one_block, running)

    return folder


def per_device(
    byte_states,
    patch_latents,
    patch_lengths,
    w_down,
    kv_gain,
    w_query,
    w_key,
    w_value,
    w_out,
    out_gain,
):
    my_rank = lax.axis_index("mp")
    tokens_here = byte_states.shape[1]
    half_rows = tokens_here // 2
    regrouped = lax.all_to_all(
        lax.all_to_all(patch_latents, "seq", split_axis=0, concat_axis=1, tiled=True),
        "mp",
        split_axis=1,
        concat_axis=2,
        tiled=True,
    )
    projected = jnp.dot(regrouped[0], w_down, preferred_element_type=jnp.float32)
    patch_normed = rms_norm(projected, kv_gain).astype(jnp.bfloat16)
    lengths = patch_lengths[0]
    starts = jnp.cumsum(lengths) - lengths
    own_rows = byte_states[0]
    local_offsets = jnp.arange(half_rows, dtype=jnp.int32)
    first_position = my_rank * tokens_here
    position_halves = jnp.stack(
        [first_position + local_offsets, first_position + half_rows + local_offsets]
    )
    queries = jnp.dot(own_rows, w_query, preferred_element_type=jnp.float32).astype(jnp.bfloat16)
    query_halves = queries.reshape(2, half_rows, HEADS, HEAD_DIM)
    initial = (
        jnp.full((2, HEADS, half_rows), NEG_FLOOR, jnp.float32),
        jnp.zeros((2, HEADS, half_rows), jnp.float32),
        jnp.zeros((2, HEADS, half_rows, HEAD_DIM), jnp.float32),
    )
    key_rows = jnp.dot(patch_normed, w_key, preferred_element_type=jnp.float32).astype(jnp.bfloat16)
    value_rows = jnp.dot(patch_normed, w_value, preferred_element_type=jnp.float32).astype(
        jnp.bfloat16
    )
    folder = make_folder(query_halves, position_halves, starts)
    row_max, denominator, accumulated = folder(
        initial,
        (
            lax.all_gather(key_rows, "mp", axis=0, tiled=True),
            lax.all_gather(value_rows, "mp", axis=0, tiled=True),
        ),
        jnp.int32(0),
    )
    summed = accumulated / denominator[..., None]
    head_out = (
        jnp.transpose(summed, (0, 2, 1, 3))
        .reshape(tokens_here, HEADS * HEAD_DIM)
        .astype(jnp.bfloat16)
    )
    residual = own_rows.astype(jnp.float32) + jnp.dot(
        head_out, w_out, preferred_element_type=jnp.float32
    )
    decoded = rms_norm(residual, out_gain).astype(jnp.bfloat16)
    return decoded[None]


def solution(mesh):
    return jax.shard_map(
        per_device,
        mesh=mesh,
        in_specs=(
            P("seq", "mp", None),
            P(None, "seq", "mp"),
            P("seq", None),
            P(),
            P(),
            P(),
            P(),
            P(),
            P(),
            P(),
        ),
        out_specs=P("seq", "mp", None),
        check_vma=False,
    )
```

profile of v0, /device:TPU:16, one launch (start us, length us, event | category | flops | bytes accessed | tf_op | source)
XLA Modules:
  0.0 283.9 jit_solution(9395675272807082795)
XLA Ops:
  6.5 18.0 %all_to_all.27 = bf16[4,256,512]{2,1,0:T(8,128)(2,1)S(1)} all-to-all(bf16[4,256,512]{2,1,0:T(8,128)(2,1)} %param.17), channel_id=1, replica_groups=mesh['seq'=4,'mp'=8] {'seq'}, dimensions={0} | all-to-all | bytes 2097152 | tf_op jit(solution)/shard_map/all_to_all | solution.py:94
  24.6 3.0 %copy.45 = bf16[1,1024,512]{2,0,1:T(2,128)(2,1)} copy(bf16[1,1024,512]{2,1,0:T(8,128)(2,1)S(1)} %bitcast.101) | data formatting | bytes 2097152 | tf_op jit(solution)/shard_map/all_to_all | solution.py:94
  28.1 8.0 %reduce.2 = bf16[1024,512]{1,0:T(8,128)(2,1)S(1)} reduce(bf16[1024,1,512]{2,1,0:T(2,128)(2,1)} %bitcast.98, bf16[]{:T(256)} %broadcast.104), dimensions={1}, to_apply=%bitcast.78.reduce_sub_computation | reduce | bytes 2097154
  36.1 1.6 reshape.138
  37.7 6.2 %all-to-all-start.1 = ((bf16[8,2,32768]{2,1,0:T(2,128)(2,1)}), bf16[8,2,32768]{2,1,0:T(2,128)(2,1)S(1)}, u32[]{:S(2)}, u32[]{:S(2)}) async-start(bf16[8,2,32768]{2,1,0:T(2,128)(2,1)} %reshape.138), calls=%async_computation.1 | async-start | bytes 2097152 | tf_op jit(solution)/shard_map/all_to_all | solution.py:93
  43.9 22.3 %all-to-all-done.1 = bf16[8,2,32768]{2,1,0:T(2,128)(2,1)S(1)} async-done(((bf16[8,2,32768]{2,1,0:T(2,128)(2,1)}), bf16[8,2,32768]{2,1,0:T(2,128)(2,1)S(1)}, u32[]{:S(2)}, u32[]{:S(2)}) %all-to-all-start.1) | async-done | bytes 1048608 | tf_op jit(solution)/shard_map/all_to_all | solution.py:93
  66.1 3.4 %reshape.139 = bf16[1024,1,512]{2,1,0:T(2,128)(2,1)} reshape(bf16[8,2,32768]{2,1,0:T(2,128)(2,1)S(1)} %all-to-all-done.1) | data formatting | bytes 2097152
  69.6 2.8 %copy.42 = bf16[1,1024,512]{2,1,0:T(8,128)(2,1)} copy(bf16[1,1024,512]{2,0,1:T(2,128)(2,1)} %bitcast.97) | data formatting | bytes 2097152
  72.4 1.6 copy.32
  74.0 4.9 %multiply_reduce_fusion.1 = (f32[128]{0:T(128)S(1)}, f32[128,1024]{1,0:T(8,128)S(1)}) fusion(bf16[128,4096]{0,1:T(8,128)(2,1)S(1)} %bitcast.99, bf16[4096,1024]{1,0:T(8,128)(2,1)} %param.19), kind=kOutput, calls=%fused_computation.58 | convolution fusion | flops 1074003840 | bytes 9961984 | tf_op jit(solution)/shard_map/dot_general | solution.py:100
  79.7 1.2 convolution_convert_fusion.2
  81.2 3.0 %convolution_convert_fusion.1 = bf16[128,1024]{1,0:T(8,128)(2,1)} fusion(bf16[1024,1024]{1,0:T(8,128)(2,1)} %param.23, f32[128,1024]{1,0:T(8,128)} %copy-done.7, f32[1024]{0:T(1024)S(1)} %convert_element_type.60, f32[128]{0:T(128)S(1)} %add_rsqrt_fusion.1), kind=kOutput, calls=%fused_computation.52 | convolution fusion | flops 268959744 | bytes 2888192 | tf_op jit(solution)/shard_map/dot_general | solution.py:118
  84.6 3.2 %convolution_convert_fusion = bf16[512,1024]{1,0:T(8,128)(2,1)S(1)} fusion(bf16[1024,1024]{1,0:T(8,128)(2,1)} %param.21, bf16[1,512,1024]{2,1,0:T(8,128)(2,1)} %param.16), kind=kOutput, calls=%fused_computation.51 | convolution fusion | flops 1074266112 | bytes 4194304 | tf_op jit(solution)/shard_map/dot_general | solution.py:110
  87.7 2.4 reshape.136
  90.1 3.6 %copy.36 = bf16[2,256,16,64]{1,3,2,0:T(8,128)(2,1)} copy(bf16[2,256,16,64]{3,2,1,0:T(8,128)(2,1)} %reshape.136) | data formatting | bytes 2097152 | tf_op jit(solution)/shard_map/while | solution.py:73
  93.8 36.8 %all-gather.3.cloned.1.call-done = bf16[1024,1024]{1,0:T(8,128)(2,1)} async-done(((bf16[128,1024]{1,0:T(8,128)(2,1)}), bf16[1024,1024]{1,0:T(8,128)(2,1)}) %all-gather.3.cloned.1.call-update) | async-done | bytes 2097168 | tf_op jit(solution)/shard_map/all_gather | solution.py:125
  130.6 49.8 %all-gather.5.cloned.1.call-done = bf16[1024,1024]{1,0:T(8,128)(2,1)} async-done(((bf16[128,1024]{1,0:T(8,128)(2,1)}), bf16[1024,1024]{1,0:T(8,128)(2,1)}) %all-gather.5.cloned.1.call-update) | async-done | bytes 2097168 | tf_op jit(solution)/shard_map/all_gather | solution.py:126
  180.4 1.6 broadcast_in_dim.57
  182.0 88.0 %while.17 = (s32[]{:T(128)}, f32[2,16,256]{2,1,0:T(8,128)S(1)}, f32[2,16,256]{2,1,0:T(8,128)S(1)}, f32[2,16,256,64]{2,3,1,0:T(8,128)}, s32[1024]{0:T(1024)S(1)},...) while((s32[]{:T(128)}, f32[2,16,256]{2,1,0:T(8,128)S(1)}, ...), condition=%wide.region_12.13_spmd, body=%wide.region_3.12_spmd.sunk | while | flops 1130135552 | bytes 103557752 | solution.py:73
  185.2 3.1 %slice_bitcast_fusion.9 = (f32[16,256,64]{1,2,0:T(8,128)}, f32[16,256,64]{1,2,0:T(8,128)}) fusion(f32[2,16,256,64]{2,3,1,0:T(8,128)} %get-tuple-element.503), kind=kLoop, calls=%fused_computation.38.clone.1 | loop fusion | bytes 4194304 | tf_op jit(solution)/shard_map/while/body/eval_jaxpr/squeeze | solution.py:54
  188.3 3.0 %constant_dynamic-slice_fusion.3 = (bf16[512,1024]{1,0:T(8,128)(2,1)}, bf16[512,1024]{1,0:T(8,128)(2,1)}) fusion(bf16[1024,1024]{1,0:T(8,128)(2,1)} %get-tuple-element.521, s32[]{:T(128)S(6)} %select_n.71, bf16[1024,1024]{1,0:T(8,128)(2,1)} %get-tuple-element.520), kind=kLoop, calls=%fused_computation.45.clone.1 | loop fusion | bytes 4194308 | tf_op jit(solution)/shard_map/while/body/eval_jaxpr/dynamic_slice | solution.py:48
  191.3 1.5 copy.48
  193.5 2.3 copy.49
  195.8 11.8 %conditional.4 = (f32[1,16,256]{2,1,0:T(8,128)}, f32[1,16,256]{2,1,0:T(8,128)S(1)}, f32[1,16,256,64]{2,3,1,0:T(8,128)}) conditional(s32[]{:T(128)} %bitcast.87, (f32[16,256]{1,0:T(8,128)}, f32[16,256]{1,0:T(8,128)S(1)}, f32[16,256,64]{1,2,0:T(8,128)}) %tuple.129, (s32[512]{0:T(512)S(1)}, s32[256]{0:T(256)S(1)}, bf16[2,256,16,64]{1,3,2,0:T(8,128)(2,1)}, ...), branch_computations={%region_8.8_spmd, %region_9.0_spmd} | conditional | flops 564797440 | bytes 43224172 | solution.py:70
  196.0 2.9 %fusion.18 = (f32[16,256]{1,0:T(8,128)S(1)}, f32[16,256,512]{2,1,0:T(8,128)S(1)}) fusion(pred[256,512]{1,0:T(8,128)(4,1)S(1)} %broadcast_compare_fusion.1, bf16[512,16,64]{0,2,1:T(8,128)(2,1)S(1)} %get-tuple-element.254, bf16[2,256,16,64]{1,3,2,0:T(8,128)(2,1)} %get-tuple-element.253), kind=kOutput, calls=%fused_computation.20 | convolution fusion | flops 274722816 | bytes 10108928 | tf_op jit(solution)/shard_map/while/body/eval_jaxpr/cond/branch_1_fun/rhd,khd->hrk/dot_general | solution.py:21
  199.5 3.2 %fusion.20 = f32[16,256]{1,0:T(8,128)S(1)} fusion(f32[16,256,512]{2,1,0:T(8,128)S(1)} %get-tuple-element.368, f32[16,256]{1,0:T(8,128)} %max.5, pred[256,512]{1,0:T(8,128)(4,1)S(1)} %broadcast_compare_fusion.1), kind=kLoop, calls=%fused_computation.22 | loop fusion | flops 10481664 | bytes 8552448 | tf_op jit(solution)/shard_map/while/body/eval_jaxpr/cond/branch_1_fun/reduce_sum | solution.py:29
  203.5 3.1 %fusion.27 = f32[1,16,256,64]{2,3,1,0:T(8,128)S(1)} fusion(bf16[512,16,64]{0,2,1:T(8,128)(2,1)S(1)} %copy-done.5, f32[16,256,512]{2,1,0:T(8,128)S(1)} %get-tuple-element.368, f32[16,256]{1,0:T(8,128)} %max.5, pred[256,512]{1,0:T(8,128)(4,1)S(1)} %broadcast_compare_fusion.1, f32[16,256,64]{1,2,0:T(8,128)S(1)} %copy-done.3, f32[16,256]{1,0:T(8,128)S(1)} %get-tuple-element.364), kind=kOutput, calls=%fused_computation.26 | convolution fusion | flops 279445504 | bytes 11698176 | tf_op jit(solution)/shard_map/while/body/eval_jaxpr/cond/branch_1_fun/hrk,khd->hrd/dot_general | solution.py:30
  210.3 11.8 %conditional.5 = (f32[1,16,256]{2,1,0:T(8,128)}, f32[1,16,256]{2,1,0:T(8,128)S(1)}, f32[1,16,256,64]{2,3,1,0:T(8,128)}) conditional(s32[]{:T(128)} %bitcast.90, (f32[16,256]{1,0:T(8,128)}, f32[16,256]{1,0:T(8,128)S(1)}, f32[16,256,64]{1,2,0:T(8,128)}) %tuple.131, (s32[512]{0:T(512)S(1)}, s32[256]{0:T(256)S(1)}, bf16[2,256,16,64]{1,3,2,0:T(8,128)(2,1)}, ...), branch_computations={%region_4.4_spmd, %region_5.0_spmd} | conditional | flops 564797440 | bytes 43224172 | solution.py:70
  210.5 2.9 %fusion = (f32[16,256]{1,0:T(8,128)S(1)}, f32[16,256,512]{2,1,0:T(8,128)S(1)}) fusion(pred[256,512]{1,0:T(8,128)(4,1)S(1)} %broadcast_compare_fusion, bf16[512,16,64]{0,2,1:T(8,128)(2,1)S(1)} %get-tuple-element.246, bf16[2,256,16,64]{1,3,2,0:T(8,128)(2,1)} %get-tuple-element.245), kind=kOutput, calls=%fused_computation.2 | convolution fusion | flops 274722816 | bytes 10108928 | tf_op jit(solution)/shard_map/while/body/eval_jaxpr/cond/branch_1_fun/rhd,khd->hrk/dot_general | solution.py:21
  214.0 3.2 %fusion.2 = f32[16,256]{1,0:T(8,128)S(1)} fusion(f32[16,256,512]{2,1,0:T(8,128)S(1)} %get-tuple-element.366, f32[16,256]{1,0:T(8,128)} %max.4, pred[256,512]{1,0:T(8,128)(4,1)S(1)} %broadcast_compare_fusion), kind=kLoop, calls=%fused_computation.4 | loop fusion | flops 10481664 | bytes 8552448 | tf_op jit(solution)/shard_map/while/body/eval_jaxpr/cond/branch_1_fun/reduce_sum | solution.py:29
  218.0 3.1 %fusion.9 = f32[1,16,256,64]{2,3,1,0:T(8,128)S(1)} fusion(bf16[512,16,64]{0,2,1:T(8,128)(2,1)S(1)} %copy-done.6, f32[16,256,512]{2,1,0:T(8,128)S(1)} %get-tuple-element.366, f32[16,256]{1,0:T(8,128)} %max.4, pred[256,512]{1,0:T(8,128)(4,1)S(1)} %broadcast_compare_fusion, f32[16,256,64]{1,2,0:T(8,128)S(1)} %copy-done.1, f32[16,256]{1,0:T(8,128)S(1)} %get-tuple-element.362), kind=kOutput, calls=%fused_computation.8 | convolution fusion | flops 279445504 | bytes 11698176 | tf_op jit(solution)/shard_map/while/body/eval_jaxpr/cond/branch_1_fun/hrk,khd->hrd/dot_general | solution.py:30
  222.9 3.1 %pad_maximum_fusion.8 = f32[2,16,256,64]{2,3,1,0:T(8,128)} fusion(f32[1,16,256,64]{2,3,1,0:T(8,128)} %get-tuple-element.472, f32[1,16,256,64]{2,3,1,0:T(8,128)} %get-tuple-element.473), kind=kLoop, calls=%fused_computation.36.clone.1 | loop fusion | flops 524288 | bytes 4194304 | tf_op jit(solution)/shard_map/while/body/eval_jaxpr/stack | solution.py:71
  229.2 3.1 %slice_bitcast_fusion.9 = (f32[16,256,64]{1,2,0:T(8,128)}, f32[16,256,64]{1,2,0:T(8,128)}) fusion(f32[2,16,256,64]{2,3,1,0:T(8,128)} %get-tuple-element.503), kind=kLoop, calls=%fused_computation.38.clone.1 | loop fusion | bytes 4194304 | tf_op jit(solution)/shard_map/while/body/eval_jaxpr/squeeze | solution.py:54
  232.3 3.0 %constant_dynamic-slice_fusion.3 = (bf16[512,1024]{1,0:T(8,128)(2,1)}, bf16[512,1024]{1,0:T(8,128)(2,1)}) fusion(bf16[1024,1024]{1,0:T(8,128)(2,1)} %get-tuple-element.521, s32[]{:T(128)S(6)} %select_n.71, bf16[1024,1024]{1,0:T(8,128)(2,1)} %get-tuple-element.520), kind=kLoop, calls=%fused_computation.45.clone.1 | loop fusion | bytes 4194308 | tf_op jit(solution)/shard_map/while/body/eval_jaxpr/dynamic_slice | solution.py:48
  235.3 1.5 copy.48
  237.5 2.3 copy.49
  239.8 11.8 %conditional.4 = (f32[1,16,256]{2,1,0:T(8,128)}, f32[1,16,256]{2,1,0:T(8,128)S(1)}, f32[1,16,256,64]{2,3,1,0:T(8,128)}) conditional(s32[]{:T(128)} %bitcast.87, (f32[16,256]{1,0:T(8,128)}, f32[16,256]{1,0:T(8,128)S(1)}, f32[16,256,64]{1,2,0:T(8,128)}) %tuple.129, (s32[512]{0:T(512)S(1)}, s32[256]{0:T(256)S(1)}, bf16[2,256,16,64]{1,3,2,0:T(8,128)(2,1)}, ...), branch_computations={%region_8.8_spmd, %region_9.0_spmd} | conditional | flops 564797440 | bytes 43224172 | solution.py:70
  240.0 2.9 %fusion.18 = (f32[16,256]{1,0:T(8,128)S(1)}, f32[16,256,512]{2,1,0:T(8,128)S(1)}) fusion(pred[256,512]{1,0:T(8,128)(4,1)S(1)} %broadcast_compare_fusion.1, bf16[512,16,64]{0,2,1:T(8,128)(2,1)S(1)} %get-tuple-element.254, bf16[2,256,16,64]{1,3,2,0:T(8,128)(2,1)} %get-tuple-element.253), kind=kOutput, calls=%fused_computation.20 | convolution fusion | flops 274722816 | bytes 10108928 | tf_op jit(solution)/shard_map/while/body/eval_jaxpr/cond/branch_1_fun/rhd,khd->hrk/dot_general | solution.py:21
  243.5 3.2 %fusion.20 = f32[16,256]{1,0:T(8,128)S(1)} fusion(f32[16,256,512]{2,1,0:T(8,128)S(1)} %get-tuple-element.368, f32[16,256]{1,0:T(8,128)} %max.5, pred[256,512]{1,0:T(8,128)(4,1)S(1)} %broadcast_compare_fusion.1), kind=kLoop, calls=%fused_computation.22 | loop fusion | flops 10481664 | bytes 8552448 | tf_op jit(solution)/shard_map/while/body/eval_jaxpr/cond/branch_1_fun/reduce_sum | solution.py:29
  247.5 3.1 %fusion.27 = f32[1,16,256,64]{2,3,1,0:T(8,128)S(1)} fusion(bf16[512,16,64]{0,2,1:T(8,128)(2,1)S(1)} %copy-done.5, f32[16,256,512]{2,1,0:T(8,128)S(1)} %get-tuple-element.368, f32[16,256]{1,0:T(8,128)} %max.5, pred[256,512]{1,0:T(8,128)(4,1)S(1)} %broadcast_compare_fusion.1, f32[16,256,64]{1,2,0:T(8,128)S(1)} %copy-done.3, f32[16,256]{1,0:T(8,128)S(1)} %get-tuple-element.364), kind=kOutput, calls=%fused_computation.26 | convolution fusion | flops 279445504 | bytes 11698176 | tf_op jit(solution)/shard_map/while/body/eval_jaxpr/cond/branch_1_fun/hrk,khd->hrd/dot_general | solution.py:30
  254.3 11.8 %conditional.5 = (f32[1,16,256]{2,1,0:T(8,128)}, f32[1,16,256]{2,1,0:T(8,128)S(1)}, f32[1,16,256,64]{2,3,1,0:T(8,128)}) conditional(s32[]{:T(128)} %bitcast.90, (f32[16,256]{1,0:T(8,128)}, f32[16,256]{1,0:T(8,128)S(1)}, f32[16,256,64]{1,2,0:T(8,128)}) %tuple.131, (s32[512]{0:T(512)S(1)}, s32[256]{0:T(256)S(1)}, bf16[2,256,16,64]{1,3,2,0:T(8,128)(2,1)}, ...), branch_computations={%region_4.4_spmd, %region_5.0_spmd} | conditional | flops 564797440 | bytes 43224172 | solution.py:70
  254.5 2.9 %fusion = (f32[16,256]{1,0:T(8,128)S(1)}, f32[16,256,512]{2,1,0:T(8,128)S(1)}) fusion(pred[256,512]{1,0:T(8,128)(4,1)S(1)} %broadcast_compare_fusion, bf16[512,16,64]{0,2,1:T(8,128)(2,1)S(1)} %get-tuple-element.246, bf16[2,256,16,64]{1,3,2,0:T(8,128)(2,1)} %get-tuple-element.245), kind=kOutput, calls=%fused_computation.2 | convolution fusion | flops 274722816 | bytes 10108928 | tf_op jit(solution)/shard_map/while/body/eval_jaxpr/cond/branch_1_fun/rhd,khd->hrk/dot_general | solution.py:21
  258.0 3.2 %fusion.2 = f32[16,256]{1,0:T(8,128)S(1)} fusion(f32[16,256,512]{2,1,0:T(8,128)S(1)} %get-tuple-element.366, f32[16,256]{1,0:T(8,128)} %max.4, pred[256,512]{1,0:T(8,128)(4,1)S(1)} %broadcast_compare_fusion), kind=kLoop, calls=%fused_computation.4 | loop fusion | flops 10481664 | bytes 8552448 | tf_op jit(solution)/shard_map/while/body/eval_jaxpr/cond/branch_1_fun/reduce_sum | solution.py:29
  262.0 3.1 %fusion.9 = f32[1,16,256,64]{2,3,1,0:T(8,128)S(1)} fusion(bf16[512,16,64]{0,2,1:T(8,128)(2,1)S(1)} %copy-done.6, f32[16,256,512]{2,1,0:T(8,128)S(1)} %get-tuple-element.366, f32[16,256]{1,0:T(8,128)} %max.4, pred[256,512]{1,0:T(8,128)(4,1)S(1)} %broadcast_compare_fusion, f32[16,256,64]{1,2,0:T(8,128)S(1)} %copy-done.1, f32[16,256]{1,0:T(8,128)S(1)} %get-tuple-element.362), kind=kOutput, calls=%fused_computation.8 | convolution fusion | flops 279445504 | bytes 11698176 | tf_op jit(solution)/shard_map/while/body/eval_jaxpr/cond/branch_1_fun/hrk,khd->hrd/dot_general | solution.py:30
  266.9 3.1 %pad_maximum_fusion.8 = f32[2,16,256,64]{2,3,1,0:T(8,128)} fusion(f32[1,16,256,64]{2,3,1,0:T(8,128)} %get-tuple-element.472, f32[1,16,256,64]{2,3,1,0:T(8,128)} %get-tuple-element.473), kind=kLoop, calls=%fused_computation.36.clone.1 | loop fusion | flops 524288 | bytes 4194304 | tf_op jit(solution)/shard_map/while/body/eval_jaxpr/stack | solution.py:71
  270.0 1.8 fusion.38
  273.2 2.6 multiply_reduce_fusion
  275.8 1.2 fusion.36
  (85 shorter events, 22.8 us)
Async XLA Ops:
  6.5 266.6 %copy-start = (bf16[1024,1024]{1,0:T(8,128)(2,1)S(1)}, bf16[1024,1024]{1,0:T(8,128)(2,1)}, u32[]{:S(2)}) copy-start(bf16[1024,1024]{1,0:T(8,128)(2,1)} %param.24) | copy-start | bytes 6291460
  6.5 37.3 %copy-start.10 = (bf16[1024]{0:T(1024)(128)(2,1)S(1)}, bf16[1024]{0:T(1024)(128)(2,1)}, u32[]{:S(2)}) copy-start(bf16[1024]{0:T(1024)(128)(2,1)} %param.20) | copy-start | bytes 6148
  37.7 28.5 %all-to-all-start.1 = ((bf16[8,2,32768]{2,1,0:T(2,128)(2,1)}), bf16[8,2,32768]{2,1,0:T(2,128)(2,1)S(1)}, u32[]{:S(2)}, u32[]{:S(2)}) async-start(bf16[8,2,32768]{2,1,0:T(2,128)(2,1)} %reshape.138), calls=%async_computation.1 | async-start | bytes 2097152 | tf_op jit(solution)/shard_map/all_to_all | solution.py:93
  43.9 86.8 %all-gather.3.cloned.1.call-start = ((), (), s32[]{:S(2)}) async-start(), calls=%async_computation.2 | async-start | bytes 2359296 | tf_op jit(solution)/shard_map/all_gather | solution.py:125
  74.0 5.7 %copy-start.8 = (bf16[1024,1024]{1,0:T(8,128)(2,1)S(1)}, bf16[1024,1024]{1,0:T(8,128)(2,1)}, u32[]{:S(2)}) copy-start(bf16[1024,1024]{1,0:T(8,128)(2,1)} %param.22) | copy-start | bytes 6291460
  74.0 10.1 %copy-start.9 = (s32[1,1024]{1,0:T(1,128)S(1)}, s32[1,1024]{1,0:T(1,128)}, u32[]{:S(2)}) copy-start(s32[1,1024]{1,0:T(1,128)} %param.18) | copy-start | bytes 12292
  78.9 0.8 copy-start.7
  80.9 12.7 %copy-start.11 = (bf16[1024]{0:T(1024)(128)(2,1)S(1)}, bf16[1024]{0:T(1024)(128)(2,1)}, u32[]{:S(2)}) copy-start(bf16[1024]{0:T(1024)(128)(2,1)} %param.25) | copy-start | bytes 6148
  80.9 99.5 %all-gather.5.cloned.1.call-start = ((), (), s32[]{:S(2)}) async-start(), calls=%async_computation.3 | async-start | bytes 2359296 | tf_op jit(solution)/shard_map/all_gather | solution.py:126
  195.9 7.5 %copy-start.3 = (f32[16,256,64]{1,2,0:T(8,128)S(1)}, f32[16,256,64]{1,2,0:T(8,128)}, u32[]{:S(2)}) copy-start(f32[16,256,64]{1,2,0:T(8,128)} %get-tuple-element.256) | copy-start | bytes 3145732 | tf_op jit(solution)/shard_map/while/body/eval_jaxpr/cond
  196.0 7.5 %copy-start.5 = (bf16[512,16,64]{0,2,1:T(8,128)(2,1)S(1)}, bf16[512,16,64]{0,2,1:T(8,128)(2,1)}, u32[]{:S(2)}) copy-start(bf16[512,16,64]{0,2,1:T(8,128)(2,1)} %get-tuple-element.257) | copy-start | bytes 3145732 | tf_op jit(solution)/shard_map/while/body/eval_jaxpr/cond
  206.6 1.0 copy-start.4
  210.5 7.5 %copy-start.1 = (f32[16,256,64]{1,2,0:T(8,128)S(1)}, f32[16,256,64]{1,2,0:T(8,128)}, u32[]{:S(2)}) copy-start(f32[16,256,64]{1,2,0:T(8,128)} %get-tuple-element.248) | copy-start | bytes 3145732 | tf_op jit(solution)/shard_map/while/body/eval_jaxpr/cond
  210.5 7.5 %copy-start.6 = (bf16[512,16,64]{0,2,1:T(8,128)(2,1)S(1)}, bf16[512,16,64]{0,2,1:T(8,128)(2,1)}, u32[]{:S(2)}) copy-start(bf16[512,16,64]{0,2,1:T(8,128)(2,1)} %get-tuple-element.249) | copy-start | bytes 3145732 | tf_op jit(solution)/shard_map/while/body/eval_jaxpr/cond
  221.2 1.0 copy-start.2
  240.0 7.5 %copy-start.3 = (f32[16,256,64]{1,2,0:T(8,128)S(1)}, f32[16,256,64]{1,2,0:T(8,128)}, u32[]{:S(2)}) copy-start(f32[16,256,64]{1,2,0:T(8,128)} %get-tuple-element.256) | copy-start | bytes 3145732 | tf_op jit(solution)/shard_map/while/body/eval_jaxpr/cond
  240.0 7.5 %copy-start.5 = (bf16[512,16,64]{0,2,1:T(8,128)(2,1)S(1)}, bf16[512,16,64]{0,2,1:T(8,128)(2,1)}, u32[]{:S(2)}) copy-start(bf16[512,16,64]{0,2,1:T(8,128)(2,1)} %get-tuple-element.257) | copy-start | bytes 3145732 | tf_op jit(solution)/shard_map/while/body/eval_jaxpr/cond
  250.7 1.0 copy-start.4
  254.5 7.5 %copy-start.1 = (f32[16,256,64]{1,2,0:T(8,128)S(1)}, f32[16,256,64]{1,2,0:T(8,128)}, u32[]{:S(2)}) copy-start(f32[16,256,64]{1,2,0:T(8,128)} %get-tuple-element.248) | copy-start | bytes 3145732 | tf_op jit(solution)/shard_map/while/body/eval_jaxpr/cond
  254.5 7.5 %copy-start.6 = (bf16[512,16,64]{0,2,1:T(8,128)(2,1)S(1)}, bf16[512,16,64]{0,2,1:T(8,128)(2,1)}, u32[]{:S(2)}) copy-start(bf16[512,16,64]{0,2,1:T(8,128)(2,1)} %get-tuple-element.249) | copy-start | bytes 3145732 | tf_op jit(solution)/shard_map/while/body/eval_jaxpr/cond
  265.2 1.0 copy-start.2
Sparse Core Ops, SparseCore 0:
  81.1 49.5 all-gather.2
  132.7 47.6 all-gather.4
where the time goes:
time: 286 us; the launch traced here: 284 us
  waiting for transfers between devices  109 us (38%)
  local copies, waits for them, and re-layouts  54.5 us (19%)
  matrix products  39.1 us (14%)
  other arithmetic  38 us (13%)
  blocking collectives  18 us (6%)
  between operations  13.5 us (5%)
  starting transfers between devices  6.39 us (2%)
  loops' own time  5.51 us (2%)
    all_gather x1, waiting for transfers between devices, per_device(): lax.all_gather(value_rows, 'mp', axis=0, tiled=True)  49.8 us
    all_gather x1, waiting for transfers between devices, per_device(): lax.all_gather(key_rows, 'mp', axis=0, tiled=True)  36.8 us
    all_to_all x1, waiting for transfers between devices, per_device(): lax.all_to_all(lax.all_to_all(patch_latents, 'seq', split_axis=0, concat_...  22.3 us
    all_to_all x1, blocking collectives, per_device(): lax.all_to_all(patch_latents, 'seq', split_axis=0, concat_axis=1, tiled=T...  18 us
    reduce_sum x4, other arithmetic, fold_block(): denominator = denominator * correction + jnp.sum(raised, axis=-1)  12.9 us
    dot_general x4, matrix products, fold_block(): jnp.einsum('hrk,khd->hrd', raised.astype(jnp.bfloat16), value_block, pref...  12.6 us
    dot_general x4, matrix products, fold_block(): jnp.einsum('rhd,khd->hrk', query_part, key_block, preferred_element_type=...  11.7 us
    another operation x10, other arithmetic, one_block(): jnp.stack([updated[0][slot], updated[1][slot]])  10.6 us
  transfers between devices with their start and end apart: 3, of which 3 were waited for; matrix products, arithmetic and copies ran while one was open for 4% of the time, Pallas kernels for 0%

commit v1 on v0

--- a/solution.py
+++ b/solution.py
@@ -90,12 +90,20 @@
     my_rank = lax.axis_index("mp")
     tokens_here = byte_states.shape[1]
     half_rows = tokens_here // 2
-    regrouped = lax.all_to_all(
-        lax.all_to_all(patch_latents, "seq", split_axis=0, concat_axis=1, tiled=True),
-        "mp",
-        split_axis=1,
-        concat_axis=2,
-        tiled=True,
+    regrouped = jnp.concatenate(
+        lax.all_to_all(
+            jnp.stack(
+                jnp.split(
+                    lax.all_to_all(patch_latents, "seq", split_axis=0, concat_axis=1, tiled=True),
+                    lax.axis_size("mp"),
+                    axis=1,
+                )
+            ),
+            "mp",
+            0,
+            0,
+        ),
+        axis=2,
     )
     projected = jnp.dot(regrouped[0], w_down, preferred_element_type=jnp.float32)
     patch_normed = rms_norm(projected, kv_gain).astype(jnp.bfloat16)

time: 286 us -> 270 us (0.944)
  other arithmetic: 38 us -> 30 us
  local copies, waits for them, and re-layouts: 54.5 us -> 47.6 us
    unnamed x1 -> x0, other arithmetic: 8.04 us -> none
    all_to_all x2 -> x0, local copies, waits for them, and re-layouts: 4.58 us -> none  [the longest x1 2.97 us: per_device(): lax.all_to_all(patch_latents, 'seq', split_axis=0, concat_axis=1, tiled=T...]
    unnamed x17 -> x28, local copies, waits for them, and re-layouts: 9.39 us -> 6.67 us
  transfers between devices with their start and end apart: 3 -> 3, of which waited for: 3 -> 3; matrix products, arithmetic and copies ran while one was open for 4% -> 5% of each run, Pallas kernels for 0% -> 0%
where the time goes in v1:
time: 270 us; the launch traced here: 269 us
  waiting for transfers between devices  109 us (40%)
  local copies, waits for them, and re-layouts  47.6 us (18%)
  matrix products  39.1 us (14%)
  other arithmetic  30 us (11%)
  blocking collectives  18 us (7%)
  between operations  13.6 us (5%)
  starting transfers between devices  6.21 us (2%)
  loops' own time  5.03 us (2%)
    all_gather x1, waiting for transfers between devices, per_device(): lax.all_gather(value_rows, 'mp', axis=0, tiled=True)  49.8 us
    all_gather x1, waiting for transfers between devices, per_device(): lax.all_gather(key_rows, 'mp', axis=0, tiled=True)  37 us
    all_to_all x1, waiting for transfers between devices, per_device(): lax.all_to_all(jnp.stack(jnp.split(lax.all_to_all(patch_latents, 'seq', s...  22.3 us
    all_to_all x1, blocking collectives, per_device(): lax.all_to_all(patch_latents, 'seq', split_axis=0, concat_axis=1, tiled=T...  18 us
    reduce_sum x4, other arithmetic, fold_block(): denominator = denominator * correction + jnp.sum(raised, axis=-1)  12.9 us
    dot_general x4, matrix products, fold_block(): jnp.einsum('hrk,khd->hrd', raised.astype(jnp.bfloat16), value_block, pref...  12.6 us
    dot_general x4, matrix products, fold_block(): jnp.einsum('rhd,khd->hrk', query_part, key_block, preferred_element_type=...  11.7 us
    another operation x10, other arithmetic, one_block(): jnp.stack([updated[0][slot], updated[1][slot]])  10.6 us
  transfers between devices with their start and end apart: 3, of which 3 were waited for; matrix products, arithmetic and copies ran while one was open for 5% of the time, Pallas kernels for 0%

profile of v1, /device:TPU:16, one launch (start us, length us, event | category | flops | bytes accessed | tf_op | source)
XLA Modules:
  0.0 268.6 jit_solution(9041626697205601930)
XLA Ops:
  6.5 18.0 %all_to_all.17 = bf16[4,256,512]{2,1,0:T(8,128)(2,1)S(1)} all-to-all(bf16[4,256,512]{2,1,0:T(8,128)(2,1)} %param.17), channel_id=1, replica_groups=mesh['seq'=4,'mp'=8] {'seq'}, dimensions={0} | all-to-all | bytes 2097152 | tf_op jit(solution)/shard_map/all_to_all | solution.py:97
  31.0 6.2 %all-to-all-start.1 = ((bf16[8,1,128,512]{2,3,1,0:T(8,128)(2,1)}), bf16[8,1,128,512]{2,3,1,0:T(8,128)(2,1)S(1)}, u32[]{:S(2)}, u32[]{:S(2)}) async-start(bf16[8,1,128,512]{2,3,1,0:T(8,128)(2,1)} %bitcast_dynamic-update-slice_fusion), calls=%async_computation.1 | async-start | bytes 2097152 | tf_op jit(solution)/shard_map/all_to_all | solution.py:94
  37.2 22.3 %all-to-all-done.1 = bf16[8,1,128,512]{2,3,1,0:T(8,128)(2,1)S(1)} async-done(((bf16[8,1,128,512]{2,3,1,0:T(8,128)(2,1)}), bf16[8,1,128,512]{2,3,1,0:T(8,128)(2,1)S(1)}, u32[]{:S(2)}, u32[]{:S(2)}) %all-to-all-start.1) | async-done | bytes 1048608 | tf_op jit(solution)/shard_map/all_to_all | solution.py:94
  59.5 4.9 %multiply_reduce_fusion.1 = (f32[128]{0:T(128)S(1)}, f32[128,1024]{1,0:T(8,128)S(1)}) fusion(bf16[128,4096]{0,1:T(8,128)(2,1)S(1)} %bitcast.110, bf16[4096,1024]{1,0:T(8,128)(2,1)} %param.19), kind=kOutput, calls=%fused_computation.58 | convolution fusion | flops 1074003840 | bytes 9961984 | tf_op jit(solution)/shard_map/dot_general | solution.py:108
  64.4 0.8 copy-done.7
  65.2 1.2 convolution_convert_fusion.2
  66.5 3.0 %convolution_convert_fusion.1 = bf16[128,1024]{1,0:T(8,128)(2,1)} fusion(bf16[1024,1024]{1,0:T(8,128)(2,1)} %param.23, f32[128,1024]{1,0:T(8,128)} %copy-done.7, f32[1024]{0:T(1024)S(1)} %convert_element_type.60, f32[128]{0:T(128)S(1)} %add_rsqrt_fusion.1), kind=kOutput, calls=%fused_computation.52 | convolution fusion | flops 268959744 | bytes 2888192 | tf_op jit(solution)/shard_map/dot_general | solution.py:126
  69.9 3.2 %convolution_convert_fusion = bf16[512,1024]{1,0:T(8,128)(2,1)S(1)} fusion(bf16[1024,1024]{1,0:T(8,128)(2,1)} %param.21, bf16[1,512,1024]{2,1,0:T(8,128)(2,1)} %param.16), kind=kOutput, calls=%fused_computation.51 | convolution fusion | flops 1074266112 | bytes 4194304 | tf_op jit(solution)/shard_map/dot_general | solution.py:118
  73.0 2.3 reshape.139
  75.4 3.6 %copy.32 = bf16[2,256,16,64]{1,3,2,0:T(8,128)(2,1)} copy(bf16[2,256,16,64]{3,2,1,0:T(8,128)(2,1)} %reshape.139) | data formatting | bytes 2097152 | tf_op jit(solution)/shard_map/while | solution.py:73
  79.1 37.0 %all-gather.3.cloned.1.call-done = bf16[1024,1024]{1,0:T(8,128)(2,1)} async-done(((bf16[128,1024]{1,0:T(8,128)(2,1)}), bf16[1024,1024]{1,0:T(8,128)(2,1)}) %all-gather.3.cloned.1.call-update) | async-done | bytes 2097168 | tf_op jit(solution)/shard_map/all_gather | solution.py:133
  116.1 49.8 %all-gather.5.cloned.1.call-done = bf16[1024,1024]{1,0:T(8,128)(2,1)} async-done(((bf16[128,1024]{1,0:T(8,128)(2,1)}), bf16[1024,1024]{1,0:T(8,128)(2,1)}) %all-gather.5.cloned.1.call-update) | async-done | bytes 2097168 | tf_op jit(solution)/shard_map/all_gather | solution.py:134
  165.9 1.6 broadcast_in_dim.57
  167.4 87.2 %while.17 = (s32[]{:T(128)}, f32[2,16,256]{2,1,0:T(8,128)S(1)}, f32[2,16,256]{2,1,0:T(8,128)S(1)}, f32[2,16,256,64]{2,3,1,0:T(8,128)}, s32[1024]{0:T(1024)S(1)},...) while((s32[]{:T(128)}, f32[2,16,256]{2,1,0:T(8,128)S(1)}, ...), condition=%wide.region_12.13_spmd, body=%wide.region_3.12_spmd.sunk | while | flops 1130135552 | bytes 103557752 | solution.py:73
  170.5 3.1 %slice_bitcast_fusion.9 = (f32[16,256,64]{1,2,0:T(8,128)}, f32[16,256,64]{1,2,0:T(8,128)}) fusion(f32[2,16,256,64]{2,3,1,0:T(8,128)} %get-tuple-element.491), kind=kLoop, calls=%fused_computation.38.clone.1 | loop fusion | bytes 4194304 | tf_op jit(solution)/shard_map/while/body/eval_jaxpr/squeeze | solution.py:54
  173.6 3.0 %constant_dynamic-slice_fusion.3 = (bf16[512,1024]{1,0:T(8,128)(2,1)}, bf16[512,1024]{1,0:T(8,128)(2,1)}) fusion(bf16[1024,1024]{1,0:T(8,128)(2,1)} %get-tuple-element.509, s32[]{:T(128)S(6)} %select_n.71, bf16[1024,1024]{1,0:T(8,128)(2,1)} %get-tuple-element.508), kind=kLoop, calls=%fused_computation.45.clone.1 | loop fusion | bytes 4194308 | tf_op jit(solution)/shard_map/while/body/eval_jaxpr/dynamic_slice | solution.py:48
  176.6 1.5 copy.50
  178.8 2.3 copy.51
  181.1 11.9 %conditional.4 = (f32[1,16,256]{2,1,0:T(8,128)}, f32[1,16,256]{2,1,0:T(8,128)S(1)}, f32[1,16,256,64]{2,3,1,0:T(8,128)}) conditional(s32[]{:T(128)} %bitcast.100, (f32[16,256]{1,0:T(8,128)}, f32[16,256]{1,0:T(8,128)S(1)}, f32[16,256,64]{1,2,0:T(8,128)}) %tuple.134, (s32[512]{0:T(512)S(1)}, s32[256]{0:T(256)S(1)}, bf16[2,256,16,64]{1,3,2,0:T(8,128)(2,1)}, ...), branch_computations={%region_8.8_spmd, %region_9.0_spmd} | conditional | flops 564797440 | bytes 43224172 | solution.py:70
  181.2 2.9 %fusion.18 = (f32[16,256]{1,0:T(8,128)S(1)}, f32[16,256,512]{2,1,0:T(8,128)S(1)}) fusion(pred[256,512]{1,0:T(8,128)(4,1)S(1)} %broadcast_compare_fusion.1, bf16[512,16,64]{0,2,1:T(8,128)(2,1)S(1)} %get-tuple-element.254, bf16[2,256,16,64]{1,3,2,0:T(8,128)(2,1)} %get-tuple-element.253), kind=kOutput, calls=%fused_computation.20 | convolution fusion | flops 274722816 | bytes 10108928 | tf_op jit(solution)/shard_map/while/body/eval_jaxpr/cond/branch_1_fun/rhd,khd->hrk/dot_general | solution.py:21
  184.8 3.2 %fusion.20 = f32[16,256]{1,0:T(8,128)S(1)} fusion(f32[16,256,512]{2,1,0:T(8,128)S(1)} %get-tuple-element.348, f32[16,256]{1,0:T(8,128)} %max.5, pred[256,512]{1,0:T(8,128)(4,1)S(1)} %broadcast_compare_fusion.1), kind=kLoop, calls=%fused_computation.22 | loop fusion | flops 10481664 | bytes 8552448 | tf_op jit(solution)/shard_map/while/body/eval_jaxpr/cond/branch_1_fun/reduce_sum | solution.py:29
  188.7 3.1 %fusion.27 = f32[1,16,256,64]{2,3,1,0:T(8,128)S(1)} fusion(bf16[512,16,64]{0,2,1:T(8,128)(2,1)S(1)} %copy-done.5, f32[16,256,512]{2,1,0:T(8,128)S(1)} %get-tuple-element.348, f32[16,256]{1,0:T(8,128)} %max.5, pred[256,512]{1,0:T(8,128)(4,1)S(1)} %broadcast_compare_fusion.1, f32[16,256,64]{1,2,0:T(8,128)S(1)} %copy-done.3, f32[16,256]{1,0:T(8,128)S(1)} %get-tuple-element.344), kind=kOutput, calls=%fused_computation.26 | convolution fusion | flops 279445504 | bytes 11698176 | tf_op jit(solution)/shard_map/while/body/eval_jaxpr/cond/branch_1_fun/hrk,khd->hrd/dot_general | solution.py:30
  191.9 1.0 copy-done.4
  195.4 11.8 %conditional.5 = (f32[1,16,256]{2,1,0:T(8,128)}, f32[1,16,256]{2,1,0:T(8,128)S(1)}, f32[1,16,256,64]{2,3,1,0:T(8,128)}) conditional(s32[]{:T(128)} %bitcast.103, (f32[16,256]{1,0:T(8,128)}, f32[16,256]{1,0:T(8,128)S(1)}, f32[16,256,64]{1,2,0:T(8,128)}) %tuple.136, (s32[512]{0:T(512)S(1)}, s32[256]{0:T(256)S(1)}, bf16[2,256,16,64]{1,3,2,0:T(8,128)(2,1)}, ...), branch_computations={%region_4.4_spmd, %region_5.0_spmd} | conditional | flops 564797440 | bytes 43224172 | solution.py:70
  195.6 2.9 %fusion = (f32[16,256]{1,0:T(8,128)S(1)}, f32[16,256,512]{2,1,0:T(8,128)S(1)}) fusion(pred[256,512]{1,0:T(8,128)(4,1)S(1)} %broadcast_compare_fusion, bf16[512,16,64]{0,2,1:T(8,128)(2,1)S(1)} %get-tuple-element.246, bf16[2,256,16,64]{1,3,2,0:T(8,128)(2,1)} %get-tuple-element.245), kind=kOutput, calls=%fused_computation.2 | convolution fusion | flops 274722816 | bytes 10108928 | tf_op jit(solution)/shard_map/while/body/eval_jaxpr/cond/branch_1_fun/rhd,khd->hrk/dot_general | solution.py:21
  199.1 3.2 %fusion.2 = f32[16,256]{1,0:T(8,128)S(1)} fusion(f32[16,256,512]{2,1,0:T(8,128)S(1)} %get-tuple-element.346, f32[16,256]{1,0:T(8,128)} %max.4, pred[256,512]{1,0:T(8,128)(4,1)S(1)} %broadcast_compare_fusion), kind=kLoop, calls=%fused_computation.4 | loop fusion | flops 10481664 | bytes 8552448 | tf_op jit(solution)/shard_map/while/body/eval_jaxpr/cond/branch_1_fun/reduce_sum | solution.py:29
  203.1 3.1 %fusion.9 = f32[1,16,256,64]{2,3,1,0:T(8,128)S(1)} fusion(bf16[512,16,64]{0,2,1:T(8,128)(2,1)S(1)} %copy-done.6, f32[16,256,512]{2,1,0:T(8,128)S(1)} %get-tuple-element.346, f32[16,256]{1,0:T(8,128)} %max.4, pred[256,512]{1,0:T(8,128)(4,1)S(1)} %broadcast_compare_fusion, f32[16,256,64]{1,2,0:T(8,128)S(1)} %copy-done.1, f32[16,256]{1,0:T(8,128)S(1)} %get-tuple-element.342), kind=kOutput, calls=%fused_computation.8 | convolution fusion | flops 279445504 | bytes 11698176 | tf_op jit(solution)/shard_map/while/body/eval_jaxpr/cond/branch_1_fun/hrk,khd->hrd/dot_general | solution.py:30
  206.2 1.0 copy-done.2
  208.0 3.1 %pad_maximum_fusion.8 = f32[2,16,256,64]{2,3,1,0:T(8,128)} fusion(f32[1,16,256,64]{2,3,1,0:T(8,128)} %get-tuple-element.460, f32[1,16,256,64]{2,3,1,0:T(8,128)} %get-tuple-element.461), kind=kLoop, calls=%fused_computation.36.clone.1 | loop fusion | flops 524288 | bytes 4194304 | tf_op jit(solution)/shard_map/while/body/eval_jaxpr/stack | solution.py:71
  214.1 3.1 %slice_bitcast_fusion.9 = (f32[16,256,64]{1,2,0:T(8,128)}, f32[16,256,64]{1,2,0:T(8,128)}) fusion(f32[2,16,256,64]{2,3,1,0:T(8,128)} %get-tuple-element.491), kind=kLoop, calls=%fused_computation.38.clone.1 | loop fusion | bytes 4194304 | tf_op jit(solution)/shard_map/while/body/eval_jaxpr/squeeze | solution.py:54
  217.2 3.0 %constant_dynamic-slice_fusion.3 = (bf16[512,1024]{1,0:T(8,128)(2,1)}, bf16[512,1024]{1,0:T(8,128)(2,1)}) fusion(bf16[1024,1024]{1,0:T(8,128)(2,1)} %get-tuple-element.509, s32[]{:T(128)S(6)} %select_n.71, bf16[1024,1024]{1,0:T(8,128)(2,1)} %get-tuple-element.508), kind=kLoop, calls=%fused_computation.45.clone.1 | loop fusion | bytes 4194308 | tf_op jit(solution)/shard_map/while/body/eval_jaxpr/dynamic_slice | solution.py:48
  220.2 1.5 copy.50
  222.4 2.3 copy.51
  224.7 11.9 %conditional.4 = (f32[1,16,256]{2,1,0:T(8,128)}, f32[1,16,256]{2,1,0:T(8,128)S(1)}, f32[1,16,256,64]{2,3,1,0:T(8,128)}) conditional(s32[]{:T(128)} %bitcast.100, (f32[16,256]{1,0:T(8,128)}, f32[16,256]{1,0:T(8,128)S(1)}, f32[16,256,64]{1,2,0:T(8,128)}) %tuple.134, (s32[512]{0:T(512)S(1)}, s32[256]{0:T(256)S(1)}, bf16[2,256,16,64]{1,3,2,0:T(8,128)(2,1)}, ...), branch_computations={%region_8.8_spmd, %region_9.0_spmd} | conditional | flops 564797440 | bytes 43224172 | solution.py:70
  224.8 2.9 %fusion.18 = (f32[16,256]{1,0:T(8,128)S(1)}, f32[16,256,512]{2,1,0:T(8,128)S(1)}) fusion(pred[256,512]{1,0:T(8,128)(4,1)S(1)} %broadcast_compare_fusion.1, bf16[512,16,64]{0,2,1:T(8,128)(2,1)S(1)} %get-tuple-element.254, bf16[2,256,16,64]{1,3,2,0:T(8,128)(2,1)} %get-tuple-element.253), kind=kOutput, calls=%fused_computation.20 | convolution fusion | flops 274722816 | bytes 10108928 | tf_op jit(solution)/shard_map/while/body/eval_jaxpr/cond/branch_1_fun/rhd,khd->hrk/dot_general | solution.py:21
  228.4 3.2 %fusion.20 = f32[16,256]{1,0:T(8,128)S(1)} fusion(f32[16,256,512]{2,1,0:T(8,128)S(1)} %get-tuple-element.348, f32[16,256]{1,0:T(8,128)} %max.5, pred[256,512]{1,0:T(8,128)(4,1)S(1)} %broadcast_compare_fusion.1), kind=kLoop, calls=%fused_computation.22 | loop fusion | flops 10481664 | bytes 8552448 | tf_op jit(solution)/shard_map/while/body/eval_jaxpr/cond/branch_1_fun/reduce_sum | solution.py:29
  232.4 3.2 %fusion.27 = f32[1,16,256,64]{2,3,1,0:T(8,128)S(1)} fusion(bf16[512,16,64]{0,2,1:T(8,128)(2,1)S(1)} %copy-done.5, f32[16,256,512]{2,1,0:T(8,128)S(1)} %get-tuple-element.348, f32[16,256]{1,0:T(8,128)} %max.5, pred[256,512]{1,0:T(8,128)(4,1)S(1)} %broadcast_compare_fusion.1, f32[16,256,64]{1,2,0:T(8,128)S(1)} %copy-done.3, f32[16,256]{1,0:T(8,128)S(1)} %get-tuple-element.344), kind=kOutput, calls=%fused_computation.26 | convolution fusion | flops 279445504 | bytes 11698176 | tf_op jit(solution)/shard_map/while/body/eval_jaxpr/cond/branch_1_fun/hrk,khd->hrd/dot_general | solution.py:30
  235.5 1.0 copy-done.4
  239.0 11.8 %conditional.5 = (f32[1,16,256]{2,1,0:T(8,128)}, f32[1,16,256]{2,1,0:T(8,128)S(1)}, f32[1,16,256,64]{2,3,1,0:T(8,128)}) conditional(s32[]{:T(128)} %bitcast.103, (f32[16,256]{1,0:T(8,128)}, f32[16,256]{1,0:T(8,128)S(1)}, f32[16,256,64]{1,2,0:T(8,128)}) %tuple.136, (s32[512]{0:T(512)S(1)}, s32[256]{0:T(256)S(1)}, bf16[2,256,16,64]{1,3,2,0:T(8,128)(2,1)}, ...), branch_computations={%region_4.4_spmd, %region_5.0_spmd} | conditional | flops 564797440 | bytes 43224172 | solution.py:70
  239.2 2.9 %fusion = (f32[16,256]{1,0:T(8,128)S(1)}, f32[16,256,512]{2,1,0:T(8,128)S(1)}) fusion(pred[256,512]{1,0:T(8,128)(4,1)S(1)} %broadcast_compare_fusion, bf16[512,16,64]{0,2,1:T(8,128)(2,1)S(1)} %get-tuple-element.246, bf16[2,256,16,64]{1,3,2,0:T(8,128)(2,1)} %get-tuple-element.245), kind=kOutput, calls=%fused_computation.2 | convolution fusion | flops 274722816 | bytes 10108928 | tf_op jit(solution)/shard_map/while/body/eval_jaxpr/cond/branch_1_fun/rhd,khd->hrk/dot_general | solution.py:21
  242.7 3.2 %fusion.2 = f32[16,256]{1,0:T(8,128)S(1)} fusion(f32[16,256,512]{2,1,0:T(8,128)S(1)} %get-tuple-element.346, f32[16,256]{1,0:T(8,128)} %max.4, pred[256,512]{1,0:T(8,128)(4,1)S(1)} %broadcast_compare_fusion), kind=kLoop, calls=%fused_computation.4 | loop fusion | flops 10481664 | bytes 8552448 | tf_op jit(solution)/shard_map/while/body/eval_jaxpr/cond/branch_1_fun/reduce_sum | solution.py:29
  246.7 3.1 %fusion.9 = f32[1,16,256,64]{2,3,1,0:T(8,128)S(1)} fusion(bf16[512,16,64]{0,2,1:T(8,128)(2,1)S(1)} %copy-done.6, f32[16,256,512]{2,1,0:T(8,128)S(1)} %get-tuple-element.346, f32[16,256]{1,0:T(8,128)} %max.4, pred[256,512]{1,0:T(8,128)(4,1)S(1)} %broadcast_compare_fusion, f32[16,256,64]{1,2,0:T(8,128)S(1)} %copy-done.1, f32[16,256]{1,0:T(8,128)S(1)} %get-tuple-element.342), kind=kOutput, calls=%fused_computation.8 | convolution fusion | flops 279445504 | bytes 11698176 | tf_op jit(solution)/shard_map/while/body/eval_jaxpr/cond/branch_1_fun/hrk,khd->hrd/dot_general | solution.py:30
  249.9 1.0 copy-done.2
  251.6 3.1 %pad_maximum_fusion.8 = f32[2,16,256,64]{2,3,1,0:T(8,128)} fusion(f32[1,16,256,64]{2,3,1,0:T(8,128)} %get-tuple-element.460, f32[1,16,256,64]{2,3,1,0:T(8,128)} %get-tuple-element.461), kind=kLoop, calls=%fused_computation.36.clone.1 | loop fusion | flops 524288 | bytes 4194304 | tf_op jit(solution)/shard_map/while/body/eval_jaxpr/stack | solution.py:71
  254.7 1.8 fusion.38
  256.5 1.1 copy.33
  257.9 2.6 multiply_reduce_fusion
  260.5 1.2 fusion.36
  (95 shorter events, 22.4 us)
Async XLA Ops:
  6.5 251.3 %copy-start = (bf16[1024,1024]{1,0:T(8,128)(2,1)S(1)}, bf16[1024,1024]{1,0:T(8,128)(2,1)}, u32[]{:S(2)}) copy-start(bf16[1024,1024]{1,0:T(8,128)(2,1)} %param.24) | copy-start | bytes 6291460
  6.5 30.7 %copy-start.10 = (bf16[1024]{0:T(1024)(128)(2,1)S(1)}, bf16[1024]{0:T(1024)(128)(2,1)}, u32[]{:S(2)}) copy-start(bf16[1024]{0:T(1024)(128)(2,1)} %param.20) | copy-start | bytes 6148
  31.0 28.5 %all-to-all-start.1 = ((bf16[8,1,128,512]{2,3,1,0:T(8,128)(2,1)}), bf16[8,1,128,512]{2,3,1,0:T(8,128)(2,1)S(1)}, u32[]{:S(2)}, u32[]{:S(2)}) async-start(bf16[8,1,128,512]{2,3,1,0:T(8,128)(2,1)} %bitcast_dynamic-update-slice_fusion), calls=%async_computation.1 | async-start | bytes 2097152 | tf_op jit(solution)/shard_map/all_to_all | solution.py:94
  37.2 78.9 %all-gather.3.cloned.1.call-start = ((), (), s32[]{:S(2)}) async-start(), calls=%async_computation.2 | async-start | bytes 2359296 | tf_op jit(solution)/shard_map/all_gather | solution.py:133
  59.5 5.7 %copy-start.8 = (bf16[1024,1024]{1,0:T(8,128)(2,1)S(1)}, bf16[1024,1024]{1,0:T(8,128)(2,1)}, u32[]{:S(2)}) copy-start(bf16[1024,1024]{1,0:T(8,128)(2,1)} %param.22) | copy-start | bytes 6291460
  59.5 10.0 %copy-start.9 = (s32[1,1024]{1,0:T(1,128)S(1)}, s32[1,1024]{1,0:T(1,128)}, u32[]{:S(2)}) copy-start(s32[1,1024]{1,0:T(1,128)} %param.18) | copy-start | bytes 12292
  64.4 0.8 copy-start.7
  66.4 12.5 %copy-start.11 = (bf16[1024]{0:T(1024)(128)(2,1)S(1)}, bf16[1024]{0:T(1024)(128)(2,1)}, u32[]{:S(2)}) copy-start(bf16[1024]{0:T(1024)(128)(2,1)} %param.25) | copy-start | bytes 6148
  66.4 99.4 %all-gather.5.cloned.1.call-start = ((), (), s32[]{:S(2)}) async-start(), calls=%async_computation.3 | async-start | bytes 2359296 | tf_op jit(solution)/shard_map/all_gather | solution.py:134
  181.2 7.5 %copy-start.3 = (f32[16,256,64]{1,2,0:T(8,128)S(1)}, f32[16,256,64]{1,2,0:T(8,128)}, u32[]{:S(2)}) copy-start(f32[16,256,64]{1,2,0:T(8,128)} %get-tuple-element.256) | copy-start | bytes 3145732 | tf_op jit(solution)/shard_map/while/body/eval_jaxpr/cond
  181.2 7.5 %copy-start.5 = (bf16[512,16,64]{0,2,1:T(8,128)(2,1)S(1)}, bf16[512,16,64]{0,2,1:T(8,128)(2,1)}, u32[]{:S(2)}) copy-start(bf16[512,16,64]{0,2,1:T(8,128)(2,1)} %get-tuple-element.257) | copy-start | bytes 3145732 | tf_op jit(solution)/shard_map/while/body/eval_jaxpr/cond
  191.9 1.0 copy-start.4
  195.5 7.5 %copy-start.1 = (f32[16,256,64]{1,2,0:T(8,128)S(1)}, f32[16,256,64]{1,2,0:T(8,128)}, u32[]{:S(2)}) copy-start(f32[16,256,64]{1,2,0:T(8,128)} %get-tuple-element.248) | copy-start | bytes 3145732 | tf_op jit(solution)/shard_map/while/body/eval_jaxpr/cond
  195.6 7.5 %copy-start.6 = (bf16[512,16,64]{0,2,1:T(8,128)(2,1)S(1)}, bf16[512,16,64]{0,2,1:T(8,128)(2,1)}, u32[]{:S(2)}) copy-start(bf16[512,16,64]{0,2,1:T(8,128)(2,1)} %get-tuple-element.249) | copy-start | bytes 3145732 | tf_op jit(solution)/shard_map/while/body/eval_jaxpr/cond
  206.2 1.0 copy-start.2
  224.8 7.5 %copy-start.3 = (f32[16,256,64]{1,2,0:T(8,128)S(1)}, f32[16,256,64]{1,2,0:T(8,128)}, u32[]{:S(2)}) copy-start(f32[16,256,64]{1,2,0:T(8,128)} %get-tuple-element.256) | copy-start | bytes 3145732 | tf_op jit(solution)/shard_map/while/body/eval_jaxpr/cond
  224.8 7.5 %copy-start.5 = (bf16[512,16,64]{0,2,1:T(8,128)(2,1)S(1)}, bf16[512,16,64]{0,2,1:T(8,128)(2,1)}, u32[]{:S(2)}) copy-start(bf16[512,16,64]{0,2,1:T(8,128)(2,1)} %get-tuple-element.257) | copy-start | bytes 3145732 | tf_op jit(solution)/shard_map/while/body/eval_jaxpr/cond
  235.5 1.0 copy-start.4
  239.2 7.5 %copy-start.1 = (f32[16,256,64]{1,2,0:T(8,128)S(1)}, f32[16,256,64]{1,2,0:T(8,128)}, u32[]{:S(2)}) copy-start(f32[16,256,64]{1,2,0:T(8,128)} %get-tuple-element.248) | copy-start | bytes 3145732 | tf_op jit(solution)/shard_map/while/body/eval_jaxpr/cond
  239.2 7.5 %copy-start.6 = (bf16[512,16,64]{0,2,1:T(8,128)(2,1)S(1)}, bf16[512,16,64]{0,2,1:T(8,128)(2,1)}, u32[]{:S(2)}) copy-start(bf16[512,16,64]{0,2,1:T(8,128)(2,1)} %get-tuple-element.249) | copy-start | bytes 3145732 | tf_op jit(solution)/shard_map/while/body/eval_jaxpr/cond
  249.9 1.0 copy-start.2
Sparse Core Ops, SparseCore 0:
  66.5 49.5 all-gather.2
  118.2 47.6 all-gather.4
